TPU v7x, 128 devices: a whole 4x4x4 slice. The times are simulated.
128 devices in a mesh: dp: 1, sp: 64 (over z, y, x), cp: 2 (over core).
Axes of the slice: x: 4, y: 4, z: 4, core: 2. Of those that a mesh axis runs over, the one named last changes fastest.
Arguments:
- x_act: bfloat16 [16, 128, 7, 2048], P('dp', 'sp', None, 'cp')
- w_one: bfloat16 [3, 3, 2048, 8192], P(None, None, 'cp')
- w_two: bfloat16 [3, 3, 8192, 2048], P(None, None, 'cp')
- bias_one: float32 [8192], replicated
Outputs:
- output: bfloat16 [16, 128, 7, 2048], P('dp', 'sp', None, 'cp')
All inputs are finite; a program needn't handle non-finite values.
Results may differ from a plain program's by a relative error of at most 0.001.
Values are sent between devices in bfloat16 or wider.
A program may use at most 1.25 GiB of HBM per device.

v0:
```python
import jax
import jax.numpy as jnp
from jax import lax
from jax.sharding import PartitionSpec as P, NamedSharding

CONV_DIMS = ("NHWC", "HWIO", "NHWC")


def solution(mesh):
    row_devs = mesh.shape["sp"]
    down_perm = [(src_dev, src_dev + 1) for src_dev in range(row_devs - 1)]
    up_perm = [(src_dev + 1, src_dev) for src_dev in range(row_devs - 1)]
    act_spec = P("dp", "sp", None, "cp")
    kernel_spec = P(None, None, "cp", None)

    def with_halo(act_tile):
        from_above = lax.ppermute(act_tile[:, -1:], "sp", down_perm)
        from_below = lax.ppermute(act_tile[:, :1], "sp", up_perm)
        return jnp.concatenate([from_above, act_tile, from_below], axis=1)

    def conv_rows(padded, kernel):
        return lax.conv_general_dilated(padded, kernel, (1, 1), ((0, 0), (1, 1)), dimension_numbers=CONV_DIMS, preferred_element_type=jnp.float32)

    def local_block(x_tile, w_one_part, w_two_part, bias_part):
        part_one = conv_rows(with_halo(x_tile), w_one_part)
        summed_one = lax.psum_scatter(part_one, "cp", scatter_dimension=3, tiled=True)
        hidden = jax.nn.relu(summed_one + bias_part).astype(jnp.bfloat16)
        part_two = conv_rows(with_halo(hidden), w_two_part)
        summed_two = lax.psum_scatter(part_two, "cp", scatter_dimension=3, tiled=True)
        return (x_tile.astype(jnp.float32) + summed_two).astype(jnp.bfloat16)

    return jax.shard_map(local_block, mesh=mesh, in_specs=(act_spec, kernel_spec, kernel_spec, P("cp")), out_specs=act_spec, check_vma=False)
```

profile of v0, /device:TPU:96, one launch (start us, length us, event | category | flops | bytes accessed | tf_op | source)
XLA Modules:
  0.0 204.0 jit_solution(15748322322703407157)
XLA Ops:
  6.5 0.0 reduce-scatter.3.cloned.1.call-start
  6.5 1.1 copy.5
  7.7 3.4 %collective-permute-start = (bf16[16,1,7,1024]{3,0,2,1:T(8,128)(2,1)S(1)}, bf16[16,1,7,1024]{3,0,2,1:T(8,128)(2,1)S(1)}, u32[]{:S(2)}, u32[]{:S(2)}) collective-permute-start(bf16[16,1,7,1024]{3,0,2,1:T(8,128)(2,1)S(1)} %get-tuple-element.7), channel_id=1, source_target_pairs={{0,2},{2,4},{4,6},{6,8},{8,10},{10,12},{12,14},{14,16},{16,18},{18... | collective-permute-start | bytes 688136 | tf_op jit(solution)/shard_map/ppermute | solution.py:17
  11.1 6.7 %collective-permute-start.1 = (bf16[16,1,7,1024]{3,0,2,1:T(8,128)(2,1)S(1)}, bf16[16,1,7,1024]{3,0,2,1:T(8,128)(2,1)S(1)}, u32[]{:S(2)}, u32[]{:S(2)}) collective-permute-start(bf16[16,1,7,1024]{3,0,2,1:T(8,128)(2,1)S(1)} %get-tuple-element.8), channel_id=1, source_target_pairs={{2,0},{4,2},{6,4},{8,6},{10,8},{12,10},{14,12},{16,14},{18,16},{20... | collective-permute-start | bytes 688136 | tf_op jit(solution)/shard_map/ppermute | solution.py:18
  17.8 4.0 %collective-permute-done = bf16[16,1,7,1024]{3,0,2,1:T(8,128)(2,1)S(1)} collective-permute-done((bf16[16,1,7,1024]{3,0,2,1:T(8,128)(2,1)S(1)}, bf16[16,1,7,1024]{3,0,2,1:T(8,128)(2,1)S(1)}, u32[]{:S(2)}, u32[]{:S(2)}) %collective-permute-start) | collective-permute-done | bytes 229408 | tf_op jit(solution)/shard_map/ppermute | solution.py:17
  21.7 1.2 collective-permute-done.1
  22.9 52.9 %fusion.6 = f32[16,2,7,8192]{3,0,2,1:T(8,128)} fusion(bf16[3,3,1024,8192]{3,2,1,0:T(8,128)(2,1)} %param.5, bf16[16,1,7,1024]{3,0,2,1:T(8,128)(2,1)S(1)} %collective-permute-done.1, bf16[16,2,7,1024]{3,0,2,1:T(8,128)(2,1)S(1)} %copy.5, bf16[16,1,7,1024]{3,0,2,1:T(8,128)(2,1)S(1)} %collective-permute-done), kind=kOutput, calls=%fused_computation.7 | convolution fusion | flops 30604394496 | bytes 159252480 | tf_op jit(solution)/shard_map/conv_general_dilated | solution.py:22
  75.9 0.0 copy-start.2
  75.9 0.0 copy-start.1
  75.9 0.0 reduce-scatter.3.cloned.1.call-update
  75.9 0.0 reduce-scatter.5.cloned.1.call-start
  76.0 0.6 copy-done.2
  76.5 0.6 dynamic-slice
  77.8 0.0 copy-done.1
  77.8 17.1 %reduce-scatter.3.cloned.1.call-done = f32[16,2,7,4096]{3,0,2,1:T(8,128)} async-done(((f32[16,2,7,8192]{3,0,2,1:T(8,128)}), f32[16,2,7,4096]{3,0,2,1:T(8,128)}) %reduce-scatter.3.cloned.1.call-update) | async-done | bytes 3670032 | tf_op jit(solution)/shard_map/reduce_scatter | solution.py:26
  94.9 2.4 %maximum_convert_fusion = bf16[16,2,7,4096]{3,0,2,1:T(8,128)(2,1)S(1)} fusion(f32[16,2,7,4096]{3,0,2,1:T(8,128)} %reduce-scatter.3.cloned.1.call-done, f32[4096]{0:T(1024)S(1)} %dynamic-slice.2), kind=kLoop, calls=%fused_computation.6 | loop fusion | flops 2752512 | bytes 5521408 | tf_op jit(solution)/shard_map/convert_element_type | solution.py:27
  97.4 0.2 fusion.14
  97.5 3.4 %collective-permute-start.2 = (bf16[16,1,7,4096]{3,0,2,1:T(8,128)(2,1)S(1)}, bf16[16,1,7,4096]{3,0,2,1:T(8,128)(2,1)S(1)}, u32[]{:S(2)}, u32[]{:S(2)}) collective-permute-start(bf16[16,1,7,4096]{3,0,2,1:T(8,128)(2,1)S(1)} %get-tuple-element.5), channel_id=1, source_target_pairs={{0,2},{2,4},{4,6},{6,8},{8,10},{10,12},{12,14},{14,16},{16,18},{18... | collective-permute-start | bytes 2752520 | tf_op jit(solution)/shard_map/ppermute | solution.py:17
  100.9 0.0 copy-start
  101.0 6.8 %collective-permute-start.3 = (bf16[16,1,7,4096]{3,0,2,1:T(8,128)(2,1)S(1)}, bf16[16,1,7,4096]{3,0,2,1:T(8,128)(2,1)}, u32[]{:S(2)}, u32[]{:S(2)}) collective-permute-start(bf16[16,1,7,4096]{3,0,2,1:T(8,128)(2,1)S(1)} %get-tuple-element.6), channel_id=1, source_target_pairs={{2,0},{4,2},{6,4},{8,6},{10,8},{12,10},{14,12},{16,14},{18,16},{20... | collective-permute-start | bytes 2752520 | tf_op jit(solution)/shard_map/ppermute | solution.py:18
  107.8 19.0 %collective-permute-done.2 = bf16[16,1,7,4096]{3,0,2,1:T(8,128)(2,1)S(1)} collective-permute-done((bf16[16,1,7,4096]{3,0,2,1:T(8,128)(2,1)S(1)}, bf16[16,1,7,4096]{3,0,2,1:T(8,128)(2,1)S(1)}, u32[]{:S(2)}, u32[]{:S(2)}) %collective-permute-start.2) | collective-permute-done | bytes 917536 | tf_op jit(solution)/shard_map/ppermute | solution.py:17
  126.7 1.3 collective-permute-done.3
  128.0 52.2 %fusion = f32[16,2,7,2048]{3,0,2,1:T(8,128)} fusion(bf16[3,3,4096,2048]{3,2,1,0:T(8,128)(2,1)} %param.6, bf16[16,1,7,4096]{3,0,2,1:T(8,128)(2,1)} %collective-permute-done.3, bf16[16,2,7,4096]{3,0,2,1:T(8,128)(2,1)S(1)} %maximum_convert_fusion, bf16[16,1,7,4096]{3,0,2,1:T(8,128)(2,1)S(1)} %collective-permute-done.2), kind=kOutput, calls=%fused_computation | convolution fusion | flops 30612652032 | bytes 156499968 | tf_op jit(solution)/shard_map/conv_general_dilated | solution.py:22
  180.2 0.0 reduce-scatter.5.cloned.1.call-update
  180.3 14.3 %reduce-scatter.5.cloned.1.call-done = f32[16,2,7,1024]{3,0,2,1:T(8,128)} async-done(((f32[16,2,7,2048]{3,0,2,1:T(8,128)}), f32[16,2,7,1024]{3,0,2,1:T(8,128)}) %reduce-scatter.5.cloned.1.call-update) | async-done | bytes 917520 | tf_op jit(solution)/shard_map/reduce_scatter | solution.py:29
  194.5 0.0 copy-done
  194.6 1.3 add_convert_fusion
  195.9 1.2 copy.9
  (2 shorter events, 0.0 us)
Async XLA Ops:
  6.5 88.4 %reduce-scatter.3.cloned.1.call-start = ((), (), s32[]{:S(2)}) async-start(), calls=%async_computation.2 | async-start | bytes 11010048 | tf_op jit(solution)/shard_map/reduce_scatter | solution.py:26
  7.7 14.0 %collective-permute-start = (bf16[16,1,7,1024]{3,0,2,1:T(8,128)(2,1)S(1)}, bf16[16,1,7,1024]{3,0,2,1:T(8,128)(2,1)S(1)}, u32[]{:S(2)}, u32[]{:S(2)}) collective-permute-start(bf16[16,1,7,1024]{3,0,2,1:T(8,128)(2,1)S(1)} %get-tuple-element.7), channel_id=1, source_target_pairs={{0,2},{2,4},{4,6},{6,8},{8,10},{10,12},{12,14},{14,16},{16,18},{18... | collective-permute-start | bytes 688136 | tf_op jit(solution)/shard_map/ppermute | solution.py:17
  11.1 11.8 %collective-permute-start.1 = (bf16[16,1,7,1024]{3,0,2,1:T(8,128)(2,1)S(1)}, bf16[16,1,7,1024]{3,0,2,1:T(8,128)(2,1)S(1)}, u32[]{:S(2)}, u32[]{:S(2)}) collective-permute-start(bf16[16,1,7,1024]{3,0,2,1:T(8,128)(2,1)S(1)} %get-tuple-element.8), channel_id=1, source_target_pairs={{2,0},{4,2},{6,4},{8,6},{10,8},{12,10},{14,12},{16,14},{18,16},{20... | collective-permute-start | bytes 688136 | tf_op jit(solution)/shard_map/ppermute | solution.py:18
  75.9 0.7 copy-start.2
  75.9 1.9 copy-start.1
  75.9 118.6 %reduce-scatter.5.cloned.1.call-start = ((), (), s32[]{:S(2)}) async-start(), calls=%async_computation.3 | async-start | bytes 2752512 | tf_op jit(solution)/shard_map/reduce_scatter | solution.py:29
  97.5 29.2 %collective-permute-start.2 = (bf16[16,1,7,4096]{3,0,2,1:T(8,128)(2,1)S(1)}, bf16[16,1,7,4096]{3,0,2,1:T(8,128)(2,1)S(1)}, u32[]{:S(2)}, u32[]{:S(2)}) collective-permute-start(bf16[16,1,7,4096]{3,0,2,1:T(8,128)(2,1)S(1)} %get-tuple-element.5), channel_id=1, source_target_pairs={{0,2},{2,4},{4,6},{6,8},{8,10},{10,12},{12,14},{14,16},{16,18},{18... | collective-permute-start | bytes 2752520 | tf_op jit(solution)/shard_map/ppermute | solution.py:17
  100.9 93.6 %copy-start = (bf16[16,2,7,1024]{3,1,2,0:T(2,128)(2,1)S(1)}, bf16[16,2,7,1024]{3,1,2,0:T(2,128)(2,1)}, u32[]{:S(2)}) copy-start(bf16[16,2,7,1024]{3,1,2,0:T(2,128)(2,1)} %param.4) | copy-start | bytes 1376260
  101.0 27.1 %collective-permute-start.3 = (bf16[16,1,7,4096]{3,0,2,1:T(8,128)(2,1)S(1)}, bf16[16,1,7,4096]{3,0,2,1:T(8,128)(2,1)}, u32[]{:S(2)}, u32[]{:S(2)}) collective-permute-start(bf16[16,1,7,4096]{3,0,2,1:T(8,128)(2,1)S(1)} %get-tuple-element.6), channel_id=1, source_target_pairs={{2,0},{4,2},{6,4},{8,6},{10,8},{12,10},{14,12},{16,14},{18,16},{20... | collective-permute-start | bytes 2752520 | tf_op jit(solution)/shard_map/ppermute | solution.py:18
Sparse Core Ops, SparseCore 0:
  76.0 18.8 reduce-scatter.2
  180.4 14.1 reduce-scatter.4
where the time goes:
time: 207 us; the launch traced here: 204 us
  matrix products  105 us (51%)
  waiting for transfers between devices  56.9 us (27%)
  starting transfers between devices  20.3 us (10%)
  between operations  14.1 us (7%)
  other arithmetic  3.75 us (2%)
  local copies, waits for them, and re-layouts  3.73 us (2%)
    conv_general_dilated x2, matrix products, conv_rows(): lax.conv_general_dilated(padded, kernel, (1, 1), ((0, 0), (1, 1)), dimens...  105 us
    ppermute x2, waiting for transfers between devices, with_halo(): from_above = lax.ppermute(act_tile[:, -1:], 'sp', down_perm)  22.9 us
    reduce_scatter x1, waiting for transfers between devices, local_block(): lax.psum_scatter(part_one, 'cp', scatter_dimension=3, tiled=True)  17.1 us
    reduce_scatter x1, waiting for transfers between devices, local_block(): lax.psum_scatter(part_two, 'cp', scatter_dimension=3, tiled=True)  14.3 us
    ppermute x2, starting transfers between devices, with_halo(): from_below = lax.ppermute(act_tile[:, :1], 'sp', up_perm)  13.5 us
    ppermute x2, starting transfers between devices, with_halo(): from_above = lax.ppermute(act_tile[:, -1:], 'sp', down_perm)  6.8 us
  transfers between devices with their start and end apart: 6, of which 6 were waited for; matrix products, arithmetic and copies ran while one was open for 0% of the time, Pallas kernels for 0%

commit v1 on v0

v1 whole, which is shorter than its diff:
```python
import functools

import jax
import jax.numpy as jnp
from jax import lax
from jax.experimental import pallas as pl
from jax.experimental.pallas import tpu as pltpu
from jax.sharding import PartitionSpec as P

IMAGES = 16
COLS = 7
ROW = COLS * IMAGES
OWN = 2 * ROW
CHUNK = 512
KBLOCK = 1024
KY_ORDER = (1, 0, 2)
MESH = pl.DeviceIdType.MESH


def resblock_kernel(sp_size, chan, hidden, x_ref, w1_ref, w2_ref, bias_ref, out_ref,
                    xbuf, abuf, wbuf, acc, send, recv1, recv2, bias_v,
                    wsem, xsem, bsem, xs_sem, xr_sem, ps_sem, pr1_sem, pr2_sem, hs_sem, hr_sem):
    c = lax.axis_index("cp")
    s = lax.axis_index("sp")
    other = 1 - c
    up = lax.rem(s + sp_size - 1, sp_size)
    down = lax.rem(s + 1, sp_size)
    has_up = s > 0
    has_down = s < sp_size - 1
    half_h = hidden // 2
    half_o = chan // 2
    n1 = half_h // CHUNK
    n2 = half_o // CHUNK
    kb2 = half_h // KBLOCK
    groups1 = 2 * n1
    groups = groups1 + 2 * n2 * kb2
    slots = wbuf.shape[0]

    def w_copy(ref, rows, cols, slot, i):
        ky = KY_ORDER[i]
        return pltpu.make_async_copy(
            ref.at[pl.ds(3 * ky, 3), pl.ds(rows, KBLOCK), pl.ds(cols, CHUNK)],
            wbuf.at[slot, i], wsem.at[slot, i])

    def fetch(g):
        slot = lax.rem(g, slots)

        @pl.when(g < groups1)
        def _():
            side = lax.rem(g, 2)
            cols = (side * c + (1 - side) * other) * half_h + (g // 2) * CHUNK
            for i in range(3):
                w_copy(w1_ref, 0, pl.multiple_of(cols, CHUNK), slot, i).start()

        @pl.when((g >= groups1) & (g < groups))
        def _():
            t = g - groups1
            m = t // kb2
            kb = lax.rem(t, kb2)
            side = m // n2
            cols = (side * c + (1 - side) * other) * half_o + lax.rem(m, n2) * CHUNK
            rows = pl.multiple_of(kb * KBLOCK, KBLOCK)
            for i in range(3):
                w_copy(w2_ref, rows, pl.multiple_of(cols, CHUNK), slot, i).start()

    def x_send(i):
        src = x_ref.at[pl.ds(i * ROW, ROW)]
        dst = xbuf.at[3 if i == 0 else 0, pl.ds(IMAGES, ROW)]
        return pltpu.make_async_remote_copy(
            src, dst, xs_sem.at[i], xr_sem.at[i],
            device_id={"sp": up if i == 0 else down}, device_id_type=MESH)

    def halo_send(i, j):
        src = abuf.at[j, 1 + i, pl.ds(IMAGES, ROW)]
        dst = abuf.at[j, 3 if i == 0 else 0, pl.ds(IMAGES, ROW)]
        return pltpu.make_async_remote_copy(
            src, dst, hs_sem.at[i, j], hr_sem.at[i, j],
            device_id={"sp": up if i == 0 else down}, device_id_type=MESH)

    def part_send(slot, dst, rsem):
        return pltpu.make_async_remote_copy(
            send.at[slot], dst, ps_sem.at[slot], rsem,
            device_id={"cp": other}, device_id_type=MESH)

    for g in range(slots):
        fetch(jnp.int32(g))
    x_copies = [pltpu.make_async_copy(x_ref.at[pl.ds(h * ROW, ROW)], xbuf.at[1 + h, pl.ds(IMAGES, ROW)], xsem.at[h]) for h in range(2)]
    for x_copy in x_copies:
        x_copy.start()
    b_copy = pltpu.make_async_copy(bias_ref, bias_v, bsem)
    b_copy.start()

    barrier = pltpu.get_barrier_semaphore()
    pl.semaphore_signal(barrier, inc=1, device_id={"sp": up}, device_id_type=MESH)
    pl.semaphore_signal(barrier, inc=1, device_id={"sp": down}, device_id_type=MESH)
    pl.semaphore_signal(barrier, inc=1, device_id={"cp": other}, device_id_type=MESH)
    pl.semaphore_wait(barrier, 3)

    @pl.when(has_up)
    def _():
        x_send(0).start()

    @pl.when(has_down)
    def _():
        x_send(1).start()

    edge = jnp.zeros((4, IMAGES, CHUNK), jnp.bfloat16)
    zero = jnp.zeros((ROW, CHUNK), jnp.bfloat16)
    for w in (0, COLS + 1):
        for k in range(n2):
            xbuf[:, pl.ds(w * IMAGES, IMAGES), pl.ds(k * CHUNK, CHUNK)] = edge
        for j in range(n1):
            abuf[j, :, pl.ds(w * IMAGES, IMAGES), :] = edge

    def clear_row(r):
        for k in range(n2):
            xbuf[r, pl.ds(IMAGES, ROW), pl.ds(k * CHUNK, CHUNK)] = zero
        for j in range(n1):
            abuf[j, r, pl.ds(IMAGES, ROW), :] = zero

    @pl.when(jnp.logical_not(has_up))
    def _():
        clear_row(0)

    @pl.when(jnp.logical_not(has_down))
    def _():
        clear_row(3)

    b_copy.wait()
    for x_copy in x_copies:
        x_copy.wait()

    def group(slot, lhs, before_halo):
        total = None
        for i in range(3):
            if i == 1:
                before_halo()
            w_copy(w1_ref, 0, 0, slot, i).wait()
            for kx in range(3):
                part = jnp.dot(lhs(KY_ORDER[i], kx), wbuf[slot, i, kx], preferred_element_type=jnp.float32)
                total = part if total is None else total + part
        return total

    def x_lhs(ky, kx):
        return xbuf[pl.ds(ky, 2), pl.ds(kx * IMAGES, ROW), :].reshape(OWN, half_o)

    def wait_x_halo():
        @pl.when(has_up)
        def _():
            x_send(1).wait_recv()

        @pl.when(has_down)
        def _():
            x_send(0).wait_recv()

    def nothing():
        pass

    def conv1_step(j, carry):
        for side in range(2):
            g = 2 * j + side

            def before():
                if side == 0:
                    pl.when(j == 0)(wait_x_halo)

            if side == 0:
                slot = lax.rem(j, 2)

                @pl.when(j >= 2)
                def _():
                    part_send(slot, recv1.at[j], pr1_sem.at[j]).wait_send()

                send[slot] = group(lax.rem(g, slots), x_lhs, before)
                fetch(g + slots)
                part_send(slot, recv1.at[j], pr1_sem.at[j]).start()
            else:
                acc[...] = group(lax.rem(g, slots), x_lhs, before)
                fetch(g + slots)
                part_send(0, recv1.at[j], pr1_sem.at[j]).wait_recv()
                brow = c * (half_h // 128) + j * (CHUNK // 128)
                for h in range(2):
                    for q in range(CHUNK // 128):
                        rows, cols = pl.ds(h * ROW, ROW), pl.ds(q * 128, 128)
                        val = acc[rows, cols] + recv1[j, rows, cols] + bias_v[pl.ds(brow + q, 1), :]
                        abuf[j, 1 + h, pl.ds(IMAGES, ROW), cols] = jnp.maximum(val, 0.0).astype(jnp.bfloat16)

                @pl.when(has_up)
                def _():
                    halo_send(0, j).start()

                @pl.when(has_down)
                def _():
                    halo_send(1, j).start()
        return carry

    lax.fori_loop(0, n1, conv1_step, 0)

    per_kb = KBLOCK // CHUNK

    def conv2_chunk(m, first_pass, dst):
        dst[...] = jnp.zeros((OWN, CHUNK), jnp.float32)

        def kb_step(kb, carry):
            g = groups1 + m * kb2 + kb

            def a_lhs(ky, kx):
                return jnp.concatenate([abuf[kb * per_kb + d, pl.ds(ky, 2), pl.ds(kx * IMAGES, ROW), :].reshape(OWN, CHUNK)
                                        for d in range(per_kb)], axis=1)

            def wait_halo():
                for d in range(per_kb):
                    @pl.when(has_up)
                    def _():
                        halo_send(1, kb * per_kb + d).wait_recv()

                    @pl.when(has_down)
                    def _():
                        halo_send(0, kb * per_kb + d).wait_recv()

            part = group(lax.rem(g, slots), a_lhs, (lambda: pl.when(m == 0)(wait_halo)) if first_pass else nothing)
            dst[...] = dst[...] + part
            fetch(g + slots)
            return carry

        lax.fori_loop(0, kb2, kb_step, 0)

    def conv2_send(m, carry):
        slot = lax.rem(m, 2)
        part_send(slot, recv2.at[m], pr2_sem.at[m]).wait_send()
        conv2_chunk(m, True, send.at[slot])
        part_send(slot, recv2.at[m], pr2_sem.at[m]).start()
        return carry

    def conv2_own(m, carry):
        conv2_chunk(n2 + m, False, acc)
        part_send(0, recv2.at[m], pr2_sem.at[m]).wait_recv()
        cols = pl.ds(pl.multiple_of(m * CHUNK, CHUNK), CHUNK)
        for h in range(2):
            rows = pl.ds(h * ROW, ROW)
            val = xbuf[1 + h, pl.ds(IMAGES, ROW), cols].astype(jnp.float32) + (acc[rows, :] + recv2[m, rows, :])
            out_ref[rows, cols] = val.astype(jnp.bfloat16)
        return carry

    lax.fori_loop(0, n2, conv2_send, 0)
    lax.fori_loop(0, n2, conv2_own, 0)

    for slot in range(2):
        part_send(slot, recv2.at[slot], pr2_sem.at[slot]).wait_send()

    @pl.when(has_up)
    def _():
        x_send(0).wait_send()
        for j in range(n1):
            halo_send(0, j).wait_send()

    @pl.when(has_down)
    def _():
        x_send(1).wait_send()
        for j in range(n1):
            halo_send(1, j).wait_send()


def solution(mesh):
    sp_size = mesh.shape["sp"]
    act_spec = P("dp", "sp", None, "cp")
    kernel_spec = P(None, None, "cp", None)

    def local_block(x_tile, w_one, w_two, bias):
        half_o = x_tile.shape[3]
        chan, hidden = 2 * half_o, w_one.shape[3]
        half_h = hidden // 2
        n1, n2 = half_h // CHUNK, half_o // CHUNK
        x_rows = x_tile.transpose(1, 2, 0, 3).reshape(OWN, half_o)
        any_spec = pl.BlockSpec(memory_space=pl.ANY)
        dma = pltpu.SemaphoreType.DMA
        out = pl.pallas_call(
            functools.partial(resblock_kernel, sp_size, chan, hidden),
            out_shape=jax.ShapeDtypeStruct((OWN, half_o), jnp.bfloat16),
            in_specs=[any_spec] * 4,
            out_specs=pl.BlockSpec(memory_space=pltpu.VMEM),
            scratch_shapes=[
                pltpu.VMEM((4, ROW + 2 * IMAGES, half_o), jnp.bfloat16),
                pltpu.VMEM((n1, 4, ROW + 2 * IMAGES, CHUNK), jnp.bfloat16),
                pltpu.VMEM((4, 3, 3, KBLOCK, CHUNK), jnp.bfloat16),
                pltpu.VMEM((OWN, CHUNK), jnp.float32),
                pltpu.VMEM((2, OWN, CHUNK), jnp.float32),
                pltpu.VMEM((n1, OWN, CHUNK), jnp.float32),
                pltpu.VMEM((n2, OWN, CHUNK), jnp.float32),
                pltpu.VMEM((hidden // 128, 128), jnp.float32),
                dma((4, 3)), dma((2,)), dma, dma((2,)), dma((2,)), dma((2,)), dma((n1,)), dma((n2,)),
                dma((2, n1)), dma((2, n1)),
            ],
            compiler_params=pltpu.CompilerParams(
                collective_id=0, has_side_effects=True, vmem_limit_bytes=60 * 1024 * 1024),
        )(x_rows, w_one.reshape(9, half_o, hidden), w_two.reshape(9, half_h, chan), bias.reshape(hidden // 128, 128))
        return out.reshape(2, COLS, IMAGES, half_o).transpose(2, 0, 1, 3)

    return jax.shard_map(local_block, mesh=mesh, in_specs=(act_spec, kernel_spec, kernel_spec, P(None)), out_specs=act_spec, check_vma=False)
```

time: 207 us -> 101 us (0.49)
  matrix products: 105 us -> 0 us
  Pallas kernels: 0 us -> 94.4 us
  waiting for transfers between devices: 56.9 us -> 0 us
  starting transfers between devices: 20.3 us -> 0 us
  between operations: 14.1 us -> 0.01 us
  other arithmetic: 3.75 us -> 0 us
    conv_general_dilated x2 -> x0, matrix products: 105 us -> none  [conv_rows(): lax.conv_general_dilated(padded, kernel, (1, 1), ((0, 0), (1, 1)), dimens...]
    pallas_call x0 -> x1, Pallas kernels: none -> 94.4 us  [local_block(): pl.pallas_call(functools.partial(resblock_kernel, sp_size, chan, hidden),...]
    reduce_scatter x2 -> x0, waiting for transfers between devices: 31.4 us -> none  [the longest x1 17.1 us: local_block(): lax.psum_scatter(part_one, 'cp', scatter_dimension=3, tiled=True)]
    ppermute x4 -> x0, waiting for transfers between devices: 25.5 us -> none  [the longest x2 22.9 us: with_halo(): from_above = lax.ppermute(act_tile[:, -1:], 'sp', down_perm)]
    ppermute x4 -> x0, starting transfers between devices: 20.3 us -> none  [the longest x2 13.5 us: with_halo(): from_below = lax.ppermute(act_tile[:, :1], 'sp', up_perm)]
    convert_element_type x2 -> x0, other arithmetic: 3.75 us -> none  [the longest x1 2.43 us: local_block(): hidden = jax.nn.relu(summed_one + bias_part).astype(jnp.bfloat16)]
    reshape x0 -> x1, local copies, waits for them, and re-layouts: none -> 2.26 us  [local_block(): return out.reshape(2, COLS, IMAGES, half_o).transpose(2, 0, 1, 3)]
  transfers between devices with their start and end apart: 6 -> 0, of which waited for: 6 -> 0; matrix products, arithmetic and copies ran while one was open for 0% -> 0% of each run, Pallas kernels for 0% -> 0%
where the time goes in v1:
time: 101 us; the launch traced here: 98.6 us
  Pallas kernels  94.4 us (93%)
  local copies, waits for them, and re-layouts  4.14 us (4%)
    pallas_call x1, Pallas kernels, local_block(): pl.pallas_call(functools.partial(resblock_kernel, sp_size, chan, hidden),...  94.4 us
    reshape x1, local copies, waits for them, and re-layouts, local_block(): return out.reshape(2, COLS, IMAGES, half_o).transpose(2, 0, 1, 3)  2.26 us

profile of v1, /device:TPU:96, one launch (start us, length us, event | category | flops | bytes accessed | tf_op | source)
XLA Modules:
  0.0 98.6 jit_solution(15263526675382740701)
XLA Ops:
  0.0 1.9 %copy.5 = bf16[2,7,16,1024]{3,2,1,0:T(8,128)(2,1)} copy(bf16[2,7,16,1024]{3,0,1,2:T(2,128)(2,1)} %bitcast.11) | data formatting | bytes 917504 | tf_op jit(solution)/shard_map/transpose | solution.py:274
  1.9 94.4 %shard_map.46 = bf16[224,1024]{1,0:T(8,128)(2,1)} custom-call(bf16[224,1024]{1,0:T(8,128)(2,1)} %bitcast.10, bf16[9,1024,8192]{2,1,0:T(8,128)(2,1)} %bitcast.2.w1_ref, bf16[9,4096,2048]{2,1,0:T(8,128)(2,1)} %bitcast.3.w2_ref, f32[64,128]{1,0:T(8,128)} %bitcast.12), custom_call_target="tpu_custom_call" | custom-call | tf_op jit(solution)/shard_map/pallas_call | solution.py:277
  96.3 2.3 %copy.8 = bf16[2,7,16,1024]{3,0,1,2:T(2,128)(2,1)} copy(bf16[2,7,16,1024]{3,2,1,0:T(8,128)(2,1)} %bitcast.9) | data formatting | bytes 917504 | tf_op jit(solution)/shard_map/reshape | solution.py:297

commit v2 on v0

v2 whole, which is shorter than its diff:
```python
import functools

import jax
import jax.numpy as jnp
from jax import lax
from jax.experimental import pallas as pl
from jax.experimental.pallas import tpu as pltpu
from jax.sharding import PartitionSpec as P

IMAGES = 16
COLS = 7
ROW = COLS * IMAGES
SIDE = ROW - IMAGES
OWN = 2 * ROW
CHUNK = 512
KBLOCK = 1024
SLOTS = 4
SOLO = 8
SHARED = 4
FIRST2 = SOLO + SHARED
LAST2 = FIRST2 + 4
GROUPS = LAST2 + 4
MESH = pl.DeviceIdType.MESH
TAPS = ((1, 0, 0, ROW), (0, 0, IMAGES, SIDE), (2, IMAGES, 0, SIDE))


def resblock_kernel(sp_size, half_o, half_h, x_ref, w1_ref, w2_ref, bias_ref, out_ref,
                    xbuf, abuf, asend, wbuf, stage, recv1, recv2, msend, mrecv, fin, bias_v,
                    wsem, xsem, bsem, xs_sem, xr_sem, ps_sem, pr1_sem, pr2_sem,
                    as_sem, ar_sem, os_sem, hs_sem, hr_sem, ms_sem, mr_sem):
    c = lax.axis_index("cp")
    s = lax.axis_index("sp")
    other = 1 - c
    p = lax.rem(s, 2)
    q = s // 2
    mate = s + 1 - 2 * p
    has_top = q > 0
    has_bot = q < sp_size // 2 - 1
    has_near = (s > 0) & (s < sp_size - 1)
    near_q = q + 2 * p - 1

    def w_copy(ref, kx, rows, cols, slot):
        return pltpu.make_async_copy(
            ref.at[:, kx, pl.ds(rows, KBLOCK), pl.ds(cols, CHUNK)], wbuf.at[slot, kx], wsem.at[slot, kx])

    def fetch(g):
        slot = lax.rem(g, SLOTS)

        @pl.when(g < FIRST2)
        def _():
            side = lax.rem(g, 2)
            unit = g // 2 + (g // SOLO) * 2 * p
            cols = (side * c + (1 - side) * other) * half_h + unit * CHUNK
            for kx, _, _, _ in TAPS:
                w_copy(w1_ref, kx, 0, pl.multiple_of(cols, CHUNK), slot).start()

        @pl.when((g >= FIRST2) & (g < GROUPS))
        def _():
            t = g - FIRST2
            m = t // 4
            r = lax.rem(t, 4)
            side = (1 - m) * lax.rem(r, 2) + m * (r // 2)
            kb = (1 - m) * (r // 2) + m * lax.rem(r, 2)
            cols = (side * c + (1 - side) * other) * half_o + m * CHUNK
            rows = kb * 2 * KBLOCK + p * KBLOCK
            for kx, _, _, _ in TAPS:
                w_copy(w2_ref, kx, pl.multiple_of(rows, KBLOCK), pl.multiple_of(cols, CHUNK), slot).start()

    def remote(src, dst, send_sem, recv_sem, device_id):
        return pltpu.make_async_remote_copy(src, dst, send_sem, recv_sem, device_id=device_id, device_id_type=MESH)

    def x_mate(i):
        row = 1 - p if i == 0 else p
        return remote(x_ref.at[pl.ds(row * ROW, ROW)], xbuf.at[1 + 2 * p + row], xs_sem.at[i], xr_sem.at[i], {"sp": mate})

    def x_outer(k):
        return remote(x_ref.at[pl.ds(p * ROW, ROW)], xbuf.at[5 * (1 - p)], xs_sem.at[2 + k], xr_sem.at[3 - p],
                      {"sp": 2 * near_q + k})

    def x_arrived(i):
        return remote(x_ref.at[pl.ds(0, ROW)], xbuf.at[0], xs_sem.at[0], xr_sem.at[i], {"sp": mate})

    def part_send(src, dst, ssem, rsem):
        return remote(src, dst, ssem, rsem, {"cp": other})

    def solo_part(u):
        return part_send(stage.at[lax.rem(u, 2), pl.ds(0, 2)], recv1.at[u], ps_sem.at[lax.rem(u, 2)], pr1_sem.at[u])

    def shared_part(t):
        return part_send(stage.at[t].reshape(2, 2, ROW, CHUNK), recv1.at[pl.ds(4 + 2 * t, 2)], ps_sem.at[t], pr1_sem.at[4 + t])

    def first2_part():
        return part_send(stage.at[0], recv2.at[0], ps_sem.at[0], pr2_sem.at[0])

    def last2_part(turn, r0):
        return part_send(stage.at[1, pl.ds(2 * turn, 2)], recv2.at[1, pl.ds(r0, 2)], ps_sem.at[1 + turn], pr2_sem.at[1 + turn])

    def unit_home(u):
        return lax.rem(u // 2, 2), (u // 4) * 2 + lax.rem(u, 2)

    def a_mate(u):
        _, j = unit_home(u)
        return remote(asend.at[u], abuf.at[j, pl.ds(1 + 2 * p, 2)], as_sem.at[u], ar_sem.at[j], {"sp": mate})

    def a_outer(u):
        k, j = unit_home(u)
        return remote(asend.at[u, p], abuf.at[j, 5 * (1 - p)], os_sem.at[u], hr_sem.at[1 - p, j], {"sp": 2 * near_q + k})

    def a_halo(i, t):
        return remote(abuf.at[2 + t, 1 + 3 * i], abuf.at[2 + t, 5 * (1 - i)], hs_sem.at[i, t], hr_sem.at[1 - i, 2 + t],
                      {"sp": lax.rem(s + sp_size + 4 * i - 2, sp_size)})

    def halo_arrived(i, j):
        return remote(abuf.at[0, 0], abuf.at[j, 5 * i], hs_sem.at[0, 0], hr_sem.at[i, j], {"sp": mate})

    def mate_sum(m):
        return remote(msend.at[m], mrecv.at[m], ms_sem.at[m], mr_sem.at[m], {"sp": mate})

    for g in range(SLOTS):
        fetch(jnp.int32(g))
    x_copies = [pltpu.make_async_copy(x_ref.at[pl.ds(h * ROW, ROW)], xbuf.at[1 + 2 * p + h], xsem.at[h]) for h in range(2)]
    for x_copy in x_copies:
        x_copy.start()
    b_copy = pltpu.make_async_copy(bias_ref, bias_v, bsem)
    b_copy.start()

    barrier = pltpu.get_barrier_semaphore()
    pl.semaphore_signal(barrier, inc=1, device_id={"cp": other}, device_id_type=MESH)
    for d in (sp_size - 2, sp_size - 1, 1, 2):
        pl.semaphore_signal(barrier, inc=1, device_id={"sp": lax.rem(s + d, sp_size)}, device_id_type=MESH)
    pl.semaphore_wait(barrier, 5)

    x_mate(0).start()

    @pl.when(has_near)
    def _():
        x_outer(1 - p).start()

    x_mate(1).start()

    @pl.when(has_near)
    def _():
        x_outer(p).start()

    zero = jnp.zeros((ROW, CHUNK), jnp.bfloat16)

    def clear_row(r):
        for k in range(half_o // CHUNK):
            xbuf[r, :, pl.ds(k * CHUNK, CHUNK)] = zero
        for j in range(4):
            abuf[j, r] = zero

    @pl.when(jnp.logical_not(has_top))
    def _():
        clear_row(0)

    @pl.when(jnp.logical_not(has_bot))
    def _():
        clear_row(5)

    b_copy.wait()
    for x_copy in x_copies:
        x_copy.wait()

    def group(slot, lhs, r0, nh, dst, d0, add, waiting=None):
        def wait():
            for kx, _, _, _ in TAPS:
                w_copy(w1_ref, kx, 0, 0, slot).wait()

        if waiting is None:
            wait()
        else:
            pl.when(waiting)(wait)
        for kx, src_col, dst_col, width in TAPS:
            total = None
            for ky in range(3):
                part = jnp.dot(lhs(r0 + ky, nh, src_col, width), wbuf[slot, kx, ky], preferred_element_type=jnp.float32)
                total = part if total is None else total + part
            total = total.reshape(nh, width, CHUNK)
            where = (pl.ds(d0, nh), pl.ds(dst_col, width), slice(None))
            if add or kx != 1:
                dst[where] = dst[where] + total
            else:
                dst[where] = total

    def x_lhs(r, nh, col, width):
        return xbuf[pl.ds(r, nh), pl.ds(col, width), :].reshape(nh * width, half_o)

    def bias_row(unit, n):
        return bias_v[pl.ds(c * (half_h // 128) + unit * (CHUNK // 128) + n, 1), :]

    def solo_step(g, carry):
        side = lax.rem(g, 2)
        u = g // 2
        dst = side * 2 + (1 - side) * lax.rem(u, 2)

        @pl.when((side == 0) & (u >= 2))
        def _():
            solo_part(u).wait_send()

        @pl.when(g == 0)
        def _():
            x_arrived(0).wait_recv()

            @pl.when(has_near)
            def _():
                x_arrived(2 + p).wait_recv()

        group(lax.rem(g, SLOTS), x_lhs, 2 * p, 2, stage.at[dst], 0, False)
        fetch(g + SLOTS)

        @pl.when(side == 0)
        def _():
            solo_part(u).start()

        @pl.when(side == 1)
        def _():
            solo_part(u).wait_recv()
            k, j = unit_home(u)
            for h in range(2):
                for n in range(CHUNK // 128):
                    cols = pl.ds(n * 128, 128)
                    val = stage[2, h, :, cols] + recv1[u, h, :, cols] + bias_row(u, n)
                    asend[u, h, :, cols] = jnp.maximum(val, 0.0).astype(jnp.bfloat16)

            @pl.when(k == p)
            def _():
                abuf[j, pl.ds(1 + 2 * p, 2)] = asend[u]

            @pl.when(k != p)
            def _():
                a_mate(u).start()

            @pl.when(has_near)
            def _():
                a_outer(u).start()
        return carry

    lax.fori_loop(0, SOLO, solo_step, 0)

    x_arrived(1).wait_recv()

    @pl.when(((p == 0) & has_bot) | ((p == 1) & has_top))
    def _():
        x_arrived(3 - p).wait_recv()

    def shared_step(i, carry):
        side = lax.rem(i, 2)
        t = i // 2
        dst = side * 2 + (1 - side) * t

        @pl.when(side == 0)
        def _():
            solo_part(t).wait_send()

        group(lax.rem(SOLO + i, SLOTS), x_lhs, 0, 4, stage.at[dst], 0, False)
        fetch(SOLO + i + SLOTS)

        @pl.when(side == 0)
        def _():
            shared_part(t).start()

        @pl.when(side == 1)
        def _():
            shared_part(t).wait_recv()
            for r in range(4):
                for n in range(CHUNK // 128):
                    cols = pl.ds(n * 128, 128)
                    val = stage[2, r, :, cols] + recv1[4 + 2 * t + r // 2, r % 2, :, cols] + bias_row(4 + 2 * p + t, n)
                    abuf[2 + t, 1 + r, :, cols] = jnp.maximum(val, 0.0).astype(jnp.bfloat16)

            @pl.when(has_top)
            def _():
                a_halo(0, t).start()

            @pl.when(has_bot)
            def _():
                a_halo(1, t).start()
        return carry

    lax.fori_loop(0, SHARED, shared_step, 0)

    def a_lhs(kb):
        def lhs(r, nh, col, width):
            return jnp.concatenate([abuf[2 * kb + d, pl.ds(r, nh), pl.ds(col, width), :].reshape(nh * width, CHUNK)
                                    for d in range(2)], axis=1)
        return lhs

    def first2_step(i, carry):
        side = lax.rem(i, 2)
        kb = i // 2
        dst = stage.at[side * 2]

        @pl.when(side == 0)
        def _():
            for d in range(2):
                j = 2 * kb + d

                @pl.when(kb == 0)
                def _():
                    remote(asend.at[0], abuf.at[j, pl.ds(1, 2)], as_sem.at[0], ar_sem.at[j], {"sp": mate}).wait_recv()

                @pl.when(has_top)
                def _():
                    halo_arrived(0, j).wait_recv()

                @pl.when(has_bot)
                def _():
                    halo_arrived(1, j).wait_recv()

        @pl.when(i == 0)
        def _():
            shared_part(0).wait_send()

        @pl.when(kb == 0)
        def _():
            dst[...] = jnp.zeros((4, ROW, CHUNK), jnp.float32)

        group(lax.rem(FIRST2 + i, SLOTS), a_lhs(kb), 0, 4, dst, 0, True)
        fetch(FIRST2 + i + SLOTS)

        @pl.when(i == 2)
        def _():
            first2_part().start()

        @pl.when(i == 3)
        def _():
            first2_part().wait_recv()
            msend[0] = stage[2, pl.ds(2 - 2 * p, 2)] + recv2[0, pl.ds(2 - 2 * p, 2)]
            mate_sum(0).start()
            fin[...] = stage[2, pl.ds(2 * p, 2)] + recv2[0, pl.ds(2 * p, 2)]
        return carry

    lax.fori_loop(0, 4, first2_step, 0)

    shared_part(1).wait_send()

    def last2_step(i, carry):
        turn = i // 4
        t = lax.rem(i, 4)
        side = t // 2
        kb = lax.rem(t, 2)
        r0 = 2 * lax.rem(p + 1 + turn, 2)
        dst = stage.at[1 + side]

        @pl.when(kb == 0)
        def _():
            dst[pl.ds(2 * turn, 2)] = jnp.zeros((2, ROW, CHUNK), jnp.float32)

        group(lax.rem(LAST2 + t, SLOTS), a_lhs(kb), r0, 2, dst, 2 * turn, True, turn == 0)

        @pl.when(t == 1)
        def _():
            last2_part(turn, r0).start()

        @pl.when(i == 3)
        def _():
            last2_part(0, r0).wait_recv()
            msend[1] = stage[2, pl.ds(0, 2)] + recv2[1, pl.ds(r0, 2)]
            mate_sum(1).start()

        def finish(m, value):
            for h in range(2):
                cols = pl.ds(m * CHUNK, CHUNK)
                total = value(h) + mrecv[m, h]
                out_ref[pl.ds(h * ROW, ROW), cols] = (xbuf[1 + 2 * p + h, :, cols].astype(jnp.float32) + total).astype(jnp.bfloat16)

        @pl.when(i == 5)
        def _():
            mate_sum(0).wait_recv()
            finish(0, lambda h: fin[h])

        @pl.when(i == 7)
        def _():
            last2_part(1, r0).wait_recv()
            mate_sum(1).wait_recv()
            finish(1, lambda h: stage[2, 2 + h] + recv2[1, r0 + h])
        return carry

    lax.fori_loop(0, 8, last2_step, 0)

    first2_part().wait_send()
    for turn in range(2):
        last2_part(turn, 0).wait_send()
    for m in range(2):
        mate_sum(m).wait_send()
        x_mate(m).wait_send()

    def drain_solo(u, carry):
        k, _ = unit_home(u)

        @pl.when(k != p)
        def _():
            a_mate(u).wait_send()

        @pl.when(has_near)
        def _():
            a_outer(u).wait_send()
        return carry

    lax.fori_loop(0, 4, drain_solo, 0)

    @pl.when(has_near)
    def _():
        for k in range(2):
            x_outer(k).wait_send()

    for i, exists in enumerate((has_top, has_bot)):
        @pl.when(exists)
        def _():
            for t in range(2):
                a_halo(i, t).wait_send()


def solution(mesh):
    sp_size = mesh.shape["sp"]
    act_spec = P("dp", "sp", None, "cp")
    kernel_spec = P(None, None, "cp", None)

    def local_block(x_tile, w_one, w_two, bias):
        half_o, half_h = x_tile.shape[3], w_two.shape[2]
        x_rows = x_tile.transpose(1, 2, 0, 3).reshape(OWN, half_o)
        any_spec = pl.BlockSpec(memory_space=pl.ANY)
        dma = pltpu.SemaphoreType.DMA
        f32, bf16 = jnp.float32, jnp.bfloat16
        out = pl.pallas_call(
            functools.partial(resblock_kernel, sp_size, half_o, half_h),
            out_shape=jax.ShapeDtypeStruct((OWN, half_o), bf16),
            in_specs=[any_spec] * 4,
            out_specs=pl.BlockSpec(memory_space=pltpu.VMEM),
            scratch_shapes=[
                pltpu.VMEM((6, ROW, half_o), bf16),
                pltpu.VMEM((4, 6, ROW, CHUNK), bf16),
                pltpu.VMEM((4, 2, ROW, CHUNK), bf16),
                pltpu.VMEM((SLOTS, 3, 3, KBLOCK, CHUNK), bf16),
                pltpu.VMEM((3, 4, ROW, CHUNK), f32),
                pltpu.VMEM((8, 2, ROW, CHUNK), f32),
                pltpu.VMEM((2, 4, ROW, CHUNK), f32),
                pltpu.VMEM((2, 2, ROW, CHUNK), f32),
                pltpu.VMEM((2, 2, ROW, CHUNK), f32),
                pltpu.VMEM((2, ROW, CHUNK), f32),
                pltpu.VMEM((2 * half_h // 128, 128), f32),
                dma((SLOTS, 3)), dma((2,)), dma, dma((4,)), dma((4,)), dma((3,)), dma((6,)), dma((3,)),
                dma((4,)), dma((2,)), dma((4,)), dma((2, 2)), dma((2, 4)), dma((2,)), dma((2,)),
            ],
            compiler_params=pltpu.CompilerParams(
                collective_id=0, has_side_effects=True, vmem_limit_bytes=58 * 1024 * 1024),
        )(x_rows, w_one, w_two, bias.reshape(2 * half_h // 128, 128))
        return out.reshape(2, COLS, IMAGES, half_o).transpose(2, 0, 1, 3)

    return jax.shard_map(local_block, mesh=mesh, in_specs=(act_spec, kernel_spec, kernel_spec, P(None)), out_specs=act_spec, check_vma=False)
```

time: 207 us -> 94.6 us (0.46)
  the two profiles are of different devices: /device:TPU:96 before, /device:TPU:0 now
where the time goes in v2:
time: 94.6 us; the launch traced here: 94.4 us
  Pallas kernels  90.3 us (95%)
  local copies, waits for them, and re-layouts  4.14 us (4%)
    pallas_call x1, Pallas kernels, local_block(): pl.pallas_call(functools.partial(resblock_kernel, sp_size, half_o, half_h...  90.3 us
    reshape x1, local copies, waits for them, and re-layouts, local_block(): return out.reshape(2, COLS, IMAGES, half_o).transpose(2, 0, 1, 3)  2.26 us

profile of v2, /device:TPU:0, one launch (start us, length us, event | category | flops | bytes accessed | tf_op | source)
XLA Modules:
  0.0 94.4 jit_solution(6372485212690390206)
XLA Ops:
  0.0 1.9 %copy.5 = bf16[2,7,16,1024]{3,2,1,0:T(8,128)(2,1)} copy(bf16[2,7,16,1024]{3,0,1,2:T(2,128)(2,1)} %bitcast.9) | data formatting | bytes 917504 | tf_op jit(solution)/shard_map/transpose | solution.py:422
  1.9 90.3 %shard_map.46 = bf16[224,1024]{1,0:T(8,128)(2,1)} custom-call(bf16[224,1024]{1,0:T(8,128)(2,1)} %bitcast.8, bf16[3,3,1024,8192]{3,2,1,0:T(8,128)(2,1)} %w1_ref.1, bf16[3,3,4096,2048]{3,2,1,0:T(8,128)(2,1)} %w2_ref.1, f32[64,128]{1,0:T(8,128)} %bitcast.10), custom_call_target="tpu_custom_call" | custom-call | tf_op jit(solution)/shard_map/pallas_call | solution.py:426
  92.1 2.3 %copy.8 = bf16[2,7,16,1024]{3,0,1,2:T(2,128)(2,1)} copy(bf16[2,7,16,1024]{3,2,1,0:T(8,128)(2,1)} %bitcast.7) | data formatting | bytes 917504 | tf_op jit(solution)/shard_map/reshape | solution.py:449

commit v3 on v2

--- a/solution.py
+++ b/solution.py
@@ -17,16 +17,15 @@
 SLOTS = 4
 SOLO = 8
 SHARED = 4
-FIRST2 = SOLO + SHARED
-LAST2 = FIRST2 + 4
-GROUPS = LAST2 + 4
+SECOND = SOLO + SHARED
+GROUPS = SECOND + 12
 MESH = pl.DeviceIdType.MESH
 TAPS = ((1, 0, 0, ROW), (0, 0, IMAGES, SIDE), (2, IMAGES, 0, SIDE))
 
 
 def resblock_kernel(sp_size, half_o, half_h, x_ref, w1_ref, w2_ref, bias_ref, out_ref,
-                    xbuf, abuf, asend, wbuf, stage, recv1, recv2, msend, mrecv, fin, bias_v,
-                    wsem, xsem, bsem, xs_sem, xr_sem, ps_sem, pr1_sem, pr2_sem,
+                    xbuf, abuf, asend, wbuf, stage, recv1, recv2, msend, mrecv, bias_v,
+                    wsem, xsem, bsem, xs_sem, xr_sem, ps_sem, pr1_sem, po_sem, pr2_sem,
                     as_sem, ar_sem, os_sem, hs_sem, hr_sem, ms_sem, mr_sem):
     c = lax.axis_index("cp")
     s = lax.axis_index("sp")
@@ -46,7 +45,7 @@
     def fetch(g):
         slot = lax.rem(g, SLOTS)
 
-        @pl.when(g < FIRST2)
+        @pl.when(g < SECOND)
         def _():
             side = lax.rem(g, 2)
             unit = g // 2 + (g // SOLO) * 2 * p
@@ -54,13 +53,12 @@
             for kx, _, _, _ in TAPS:
                 w_copy(w1_ref, kx, 0, pl.multiple_of(cols, CHUNK), slot).start()
 
-        @pl.when((g >= FIRST2) & (g < GROUPS))
-        def _():
-            t = g - FIRST2
-            m = t // 4
-            r = lax.rem(t, 4)
-            side = (1 - m) * lax.rem(r, 2) + m * (r // 2)
-            kb = (1 - m) * (r // 2) + m * lax.rem(r, 2)
+        @pl.when((g >= SECOND) & (g < GROUPS))
+        def _():
+            t = g - SECOND
+            kb = lax.rem(t // 4, 2)
+            m = lax.rem(t, 4) // 2
+            side = lax.rem(t, 2)
             cols = (side * c + (1 - side) * other) * half_o + m * CHUNK
             rows = kb * 2 * KBLOCK + p * KBLOCK
             for kx, _, _, _ in TAPS:
@@ -89,11 +87,8 @@
     def shared_part(t):
         return part_send(stage.at[t].reshape(2, 2, ROW, CHUNK), recv1.at[pl.ds(4 + 2 * t, 2)], ps_sem.at[t], pr1_sem.at[4 + t])
 
-    def first2_part():
-        return part_send(stage.at[0], recv2.at[0], ps_sem.at[0], pr2_sem.at[0])
-
-    def last2_part(turn, r0):
-        return part_send(stage.at[1, pl.ds(2 * turn, 2)], recv2.at[1, pl.ds(r0, 2)], ps_sem.at[1 + turn], pr2_sem.at[1 + turn])
+    def out_part(turn, m, r0):
+        return part_send(stage.at[m, pl.ds(2 * turn, 2)], recv2.at[m, pl.ds(r0, 2)], po_sem.at[turn, m], pr2_sem.at[turn, m])
 
     def unit_home(u):
         return lax.rem(u // 2, 2), (u // 4) * 2 + lax.rem(u, 2)
@@ -124,11 +119,25 @@
     b_copy = pltpu.make_async_copy(bias_ref, bias_v, bsem)
     b_copy.start()
 
+    has_far = ((p == 0) & has_bot) | ((p == 1) & has_top)
     barrier = pltpu.get_barrier_semaphore()
-    pl.semaphore_signal(barrier, inc=1, device_id={"cp": other}, device_id_type=MESH)
-    for d in (sp_size - 2, sp_size - 1, 1, 2):
-        pl.semaphore_signal(barrier, inc=1, device_id={"sp": lax.rem(s + d, sp_size)}, device_id_type=MESH)
-    pl.semaphore_wait(barrier, 5)
+
+    def greet(device_id):
+        pl.semaphore_signal(barrier, inc=1, device_id=device_id, device_id_type=MESH)
+
+    greet({"cp": other})
+    greet({"sp": mate})
+
+    @pl.when(has_near)
+    def _():
+        for k in range(2):
+            greet({"sp": 2 * near_q + k})
+
+    @pl.when(has_far)
+    def _():
+        greet({"sp": s + 2 - 4 * p})
+
+    pl.semaphore_wait(barrier, 2 + 2 * has_near.astype(jnp.int32) + has_far.astype(jnp.int32))
 
     x_mate(0).start()
 
@@ -240,7 +249,7 @@
 
     x_arrived(1).wait_recv()
 
-    @pl.when(((p == 0) & has_bot) | ((p == 1) & has_top))
+    @pl.when(has_far)
     def _():
         x_arrived(3 - p).wait_recv()
 
@@ -286,103 +295,72 @@
                                     for d in range(2)], axis=1)
         return lhs
 
-    def first2_step(i, carry):
-        side = lax.rem(i, 2)
-        kb = i // 2
-        dst = stage.at[side * 2]
-
-        @pl.when(side == 0)
-        def _():
-            for d in range(2):
-                j = 2 * kb + d
-
-                @pl.when(kb == 0)
-                def _():
-                    remote(asend.at[0], abuf.at[j, pl.ds(1, 2)], as_sem.at[0], ar_sem.at[j], {"sp": mate}).wait_recv()
-
-                @pl.when(has_top)
-                def _():
-                    halo_arrived(0, j).wait_recv()
-
-                @pl.when(has_bot)
-                def _():
-                    halo_arrived(1, j).wait_recv()
-
-        @pl.when(i == 0)
-        def _():
-            shared_part(0).wait_send()
-
-        @pl.when(kb == 0)
-        def _():
-            dst[...] = jnp.zeros((4, ROW, CHUNK), jnp.float32)
-
-        group(lax.rem(FIRST2 + i, SLOTS), a_lhs(kb), 0, 4, dst, 0, True)
-        fetch(FIRST2 + i + SLOTS)
-
-        @pl.when(i == 2)
-        def _():
-            first2_part().start()
-
-        @pl.when(i == 3)
-        def _():
-            first2_part().wait_recv()
-            msend[0] = stage[2, pl.ds(2 - 2 * p, 2)] + recv2[0, pl.ds(2 - 2 * p, 2)]
-            mate_sum(0).start()
-            fin[...] = stage[2, pl.ds(2 * p, 2)] + recv2[0, pl.ds(2 * p, 2)]
+    def wait_a(kb):
+        for d in range(2):
+            j = 2 * kb + d
+            if kb == 0:
+                remote(asend.at[0], abuf.at[j, pl.ds(1, 2)], as_sem.at[0], ar_sem.at[j], {"sp": mate}).wait_recv()
+
+            @pl.when(has_top)
+            def _():
+                halo_arrived(0, j).wait_recv()
+
+            @pl.when(has_bot)
+            def _():
+                halo_arrived(1, j).wait_recv()
+
+    for t in range(2):
+        shared_part(t).wait_send()
+    stage[...] = jnp.zeros((4, 4, ROW, CHUNK), jnp.float32)
+
+    def second_step(i, carry):
+        turn = i // 8
+        t = lax.rem(i, 4)
+        last = lax.rem(i // 4, 2)
+        kb = lax.rem(turn + last, 2)
+        m = t // 2
+        side = lax.rem(t, 2)
+        r0 = 2 * lax.rem(p + 1 + turn, 2)
+        g = SECOND + i - 4 * turn
+
+        for k in range(2):
+            @pl.when(i == 4 * k)
+            def _():
+                wait_a(k)
+
+        group(lax.rem(g, SLOTS), a_lhs(kb), r0, 2, stage.at[2 * side + m], 2 * turn, True, i // 4 != 2)
+
+        @pl.when(i // 4 != 1)
+        def _():
+            fetch(g + SLOTS)
+
+        @pl.when((last == 1) & (side == 0))
+        def _():
+            out_part(turn, m, r0).start()
+
+        @pl.when((last == 1) & (side == 1))
+        def _():
+            out_part(turn, m, r0).wait_recv()
+
+            @pl.when(turn == 0)
+            def _():
+                msend[m] = stage[2 + m, pl.ds(0, 2)] + recv2[m, pl.ds(r0, 2)]
+                mate_sum(m).start()
+
+            @pl.when(turn == 1)
+            def _():
+                mate_sum(m).wait_recv()
+                cols = pl.ds(pl.multiple_of(m * CHUNK, CHUNK), CHUNK)
+                for h in range(2):
+                    total = stage[2 + m, 2 + h] + recv2[m, r0 + h] + mrecv[m, h]
+                    out_ref[pl.ds(h * ROW, ROW), cols] = (xbuf[1 + 2 * p + h, :, cols].astype(jnp.float32) + total).astype(jnp.bfloat16)
         return carry
 
-    lax.fori_loop(0, 4, first2_step, 0)
-
-    shared_part(1).wait_send()
-
-    def last2_step(i, carry):
-        turn = i // 4
-        t = lax.rem(i, 4)
-        side = t // 2
-        kb = lax.rem(t, 2)
-        r0 = 2 * lax.rem(p + 1 + turn, 2)
-        dst = stage.at[1 + side]
-
-        @pl.when(kb == 0)
-        def _():
-            dst[pl.ds(2 * turn, 2)] = jnp.zeros((2, ROW, CHUNK), jnp.float32)
-
-        group(lax.rem(LAST2 + t, SLOTS), a_lhs(kb), r0, 2, dst, 2 * turn, True, turn == 0)
-
-        @pl.when(t == 1)
-        def _():
-            last2_part(turn, r0).start()
-
-        @pl.when(i == 3)
-        def _():
-            last2_part(0, r0).wait_recv()
-            msend[1] = stage[2, pl.ds(0, 2)] + recv2[1, pl.ds(r0, 2)]
-            mate_sum(1).start()
-
-        def finish(m, value):
-            for h in range(2):
-                cols = pl.ds(m * CHUNK, CHUNK)
-                total = value(h) + mrecv[m, h]
-                out_ref[pl.ds(h * ROW, ROW), cols] = (xbuf[1 + 2 * p + h, :, cols].astype(jnp.float32) + total).astype(jnp.bfloat16)
-
-        @pl.when(i == 5)
-        def _():
-            mate_sum(0).wait_recv()
-            finish(0, lambda h: fin[h])
-
-        @pl.when(i == 7)
-        def _():
-            last2_part(1, r0).wait_recv()
-            mate_sum(1).wait_recv()
-            finish(1, lambda h: stage[2, 2 + h] + recv2[1, r0 + h])
-        return carry
-
-    lax.fori_loop(0, 8, last2_step, 0)
-
-    first2_part().wait_send()
-    for turn in range(2):
-        last2_part(turn, 0).wait_send()
+    lax.fori_loop(0, 16, second_step, 0)
+
     for m in range(2):
+        for turn in range(2):
+            out_part(turn, m, 0).wait_send()
         mate_sum(m).wait_send()
         x_mate(m).wait_send()
 
@@ -433,18 +411,17 @@
                 pltpu.VMEM((4, 6, ROW, CHUNK), bf16),
                 pltpu.VMEM((4, 2, ROW, CHUNK), bf16),
                 pltpu.VMEM((SLOTS, 3, 3, KBLOCK, CHUNK), bf16),
-                pltpu.VMEM((3, 4, ROW, CHUNK), f32),
+                pltpu.VMEM((4, 4, ROW, CHUNK), f32),
                 pltpu.VMEM((8, 2, ROW, CHUNK), f32),
                 pltpu.VMEM((2, 4, ROW, CHUNK), f32),
                 pltpu.VMEM((2, 2, ROW, CHUNK), f32),
                 pltpu.VMEM((2, 2, ROW, CHUNK), f32),
-                pltpu.VMEM((2, ROW, CHUNK), f32),
                 pltpu.VMEM((2 * half_h // 128, 128), f32),
-                dma((SLOTS, 3)), dma((2,)), dma, dma((4,)), dma((4,)), dma((3,)), dma((6,)), dma((3,)),
+                dma((SLOTS, 3)), dma((2,)), dma, dma((4,)), dma((4,)), dma((2,)), dma((6,)), dma((2, 2)), dma((2, 2)),
                 dma((4,)), dma((2,)), dma((4,)), dma((2, 2)), dma((2, 4)), dma((2,)), dma((2,)),
             ],
             compiler_params=pltpu.CompilerParams(
-                collective_id=0, has_side_effects=True, vmem_limit_bytes=58 * 1024 * 1024),
+                collective_id=0, has_side_effects=True, vmem_limit_bytes=53 * 1024 * 1024),
         )(x_rows, w_one, w_two, bias.reshape(2 * half_h // 128, 128))
         return out.reshape(2, COLS, IMAGES, half_o).transpose(2, 0, 1, 3)
 

time: 94.6 us -> 87.9 us (0.929)
  the two profiles are of different devices: /device:TPU:0 before, /device:TPU:96 now
where the time goes in v3:
time: 87.9 us; the launch traced here: 87.6 us
  Pallas kernels  84.5 us (96%)
  local copies, waits for them, and re-layouts  3.1 us (4%)
    pallas_call x1, Pallas kernels, local_block(): pl.pallas_call(functools.partial(resblock_kernel, sp_size, half_o, half_h...  84.5 us

profile of v3, /device:TPU:96, one launch (start us, length us, event | category | flops | bytes accessed | tf_op | source)
XLA Modules:
  0.0 87.6 jit_solution(15630746193431398042)
XLA Ops:
  0.0 1.1 %copy.5 = bf16[2,7,16,1024]{3,2,1,0:T(8,128)(2,1)S(1)} copy(bf16[2,7,16,1024]{3,0,1,2:T(2,128)(2,1)} %bitcast.10) | data formatting | bytes 917504 | tf_op jit(solution)/shard_map/transpose | solution.py:400
  1.1 0.0 copy-start
  1.1 0.7 copy-done
  1.9 84.5 %shard_map.46 = bf16[224,1024]{1,0:T(8,128)(2,1)S(1)} custom-call(bf16[224,1024]{1,0:T(8,128)(2,1)S(1)} %bitcast.8, bf16[3,3,1024,8192]{3,2,1,0:T(8,128)(2,1)} %w1_ref.1, bf16[3,3,4096,2048]{3,2,1,0:T(8,128)(2,1)} %w2_ref.1, f32[64,128]{1,0:T(8,128)S(1)} %bitcast.9), custom_call_target="tpu_custom_call" | custom-call | tf_op jit(solution)/shard_map/pallas_call | solution.py:404
  86.3 1.2 %copy.8 = bf16[2,7,16,1024]{3,0,1,2:T(2,128)(2,1)} copy(bf16[2,7,16,1024]{3,2,1,0:T(8,128)(2,1)S(1)} %bitcast.7) | data formatting | bytes 917504 | tf_op jit(solution)/shard_map/reshape | solution.py:426
Async XLA Ops:
  1.1 0.8 copy-start

commit v4 on v3

--- a/solution.py
+++ b/solution.py
@@ -15,8 +15,9 @@
 CHUNK = 512
 KBLOCK = 1024
 SLOTS = 4
-SOLO = 8
-SHARED = 4
+SOLO = 4
+SHARED = 6
+UNITS = 4
 SECOND = SOLO + SHARED
 GROUPS = SECOND + 12
 MESH = pl.DeviceIdType.MESH
@@ -48,7 +49,9 @@
         @pl.when(g < SECOND)
         def _():
             side = lax.rem(g, 2)
-            unit = g // 2 + (g // SOLO) * 2 * p
+            u = g // 2
+            shared = (g + SECOND - SOLO) // SECOND
+            unit = (1 - shared) * (UNITS * lax.rem(u, 2) + u // 2) + shared * (UNITS * p + u - SOLO // 4)
             cols = (side * c + (1 - side) * other) * half_h + unit * CHUNK
             for kx, _, _, _ in TAPS:
                 w_copy(w1_ref, kx, 0, pl.multiple_of(cols, CHUNK), slot).start()
@@ -60,7 +63,7 @@
             m = lax.rem(t, 4) // 2
             side = lax.rem(t, 2)
             cols = (side * c + (1 - side) * other) * half_o + m * CHUNK
-            rows = kb * 2 * KBLOCK + p * KBLOCK
+            rows = p * 2 * KBLOCK + kb * KBLOCK
             for kx, _, _, _ in TAPS:
                 w_copy(w2_ref, kx, pl.multiple_of(rows, KBLOCK), pl.multiple_of(cols, CHUNK), slot).start()
 
@@ -85,13 +88,15 @@
         return part_send(stage.at[lax.rem(u, 2), pl.ds(0, 2)], recv1.at[u], ps_sem.at[lax.rem(u, 2)], pr1_sem.at[u])
 
     def shared_part(t):
-        return part_send(stage.at[t].reshape(2, 2, ROW, CHUNK), recv1.at[pl.ds(4 + 2 * t, 2)], ps_sem.at[t], pr1_sem.at[4 + t])
+        slot = lax.rem(t, 2)
+        return part_send(stage.at[slot].reshape(2, 2, ROW, CHUNK), recv1.at[pl.ds(SOLO // 2 + 2 * t, 2)],
+                         ps_sem.at[slot], pr1_sem.at[SOLO // 2 + t])
 
     def out_part(turn, m, r0):
         return part_send(stage.at[m, pl.ds(2 * turn, 2)], recv2.at[m, pl.ds(r0, 2)], po_sem.at[turn, m], pr2_sem.at[turn, m])
 
     def unit_home(u):
-        return lax.rem(u // 2, 2), (u // 4) * 2 + lax.rem(u, 2)
+        return lax.rem(u, 2), u // 2
 
     def a_mate(u):
         _, j = unit_home(u)
@@ -102,7 +107,8 @@
         return remote(asend.at[u, p], abuf.at[j, 5 * (1 - p)], os_sem.at[u], hr_sem.at[1 - p, j], {"sp": 2 * near_q + k})
 
     def a_halo(i, t):
-        return remote(abuf.at[2 + t, 1 + 3 * i], abuf.at[2 + t, 5 * (1 - i)], hs_sem.at[i, t], hr_sem.at[1 - i, 2 + t],
+        j = SOLO // 4 + t
+        return remote(abuf.at[j, 1 + 3 * i], abuf.at[j, 5 * (1 - i)], hs_sem.at[i, t], hr_sem.at[1 - i, j],
                       {"sp": lax.rem(s + sp_size + 4 * i - 2, sp_size)})
 
     def halo_arrived(i, j):
@@ -201,11 +207,7 @@
     def solo_step(g, carry):
         side = lax.rem(g, 2)
         u = g // 2
-        dst = side * 2 + (1 - side) * lax.rem(u, 2)
-
-        @pl.when((side == 0) & (u >= 2))
-        def _():
-            solo_part(u).wait_send()
+        dst = side * 2 + (1 - side) * u
 
         @pl.when(g == 0)
         def _():
@@ -229,7 +231,7 @@
             for h in range(2):
                 for n in range(CHUNK // 128):
                     cols = pl.ds(n * 128, 128)
-                    val = stage[2, h, :, cols] + recv1[u, h, :, cols] + bias_row(u, n)
+                    val = stage[2, h, :, cols] + recv1[u, h, :, cols] + bias_row(UNITS * k + j, n)
                     asend[u, h, :, cols] = jnp.maximum(val, 0.0).astype(jnp.bfloat16)
 
             @pl.when(k == p)
@@ -256,11 +258,15 @@
     def shared_step(i, carry):
         side = lax.rem(i, 2)
         t = i // 2
-        dst = side * 2 + (1 - side) * t
-
-        @pl.when(side == 0)
+        dst = side * 2 + (1 - side) * lax.rem(t, 2)
+
+        @pl.when((side == 0) & (t < 2))
         def _():
             solo_part(t).wait_send()
+
+        @pl.when((side == 0) & (t >= 2))
+        def _():
+            shared_part(t).wait_send()
 
         group(lax.rem(SOLO + i, SLOTS), x_lhs, 0, 4, stage.at[dst], 0, False)
         fetch(SOLO + i + SLOTS)
@@ -275,8 +281,8 @@
             for r in range(4):
                 for n in range(CHUNK // 128):
                     cols = pl.ds(n * 128, 128)
-                    val = stage[2, r, :, cols] + recv1[4 + 2 * t + r // 2, r % 2, :, cols] + bias_row(4 + 2 * p + t, n)
-                    abuf[2 + t, 1 + r, :, cols] = jnp.maximum(val, 0.0).astype(jnp.bfloat16)
+                    val = stage[2, r, :, cols] + recv1[SOLO // 2 + 2 * t + r // 2, r % 2, :, cols] + bias_row(UNITS * p + SOLO // 4 + t, n)
+                    abuf[SOLO // 4 + t, 1 + r, :, cols] = jnp.maximum(val, 0.0).astype(jnp.bfloat16)
 
             @pl.when(has_top)
             def _():
@@ -298,7 +304,7 @@
     def wait_a(kb):
         for d in range(2):
             j = 2 * kb + d
-            if kb == 0:
+            if j < SOLO // 4:
                 remote(asend.at[0], abuf.at[j, pl.ds(1, 2)], as_sem.at[0], ar_sem.at[j], {"sp": mate}).wait_recv()
 
             @pl.when(has_top)
@@ -309,8 +315,8 @@
             def _():
                 halo_arrived(1, j).wait_recv()
 
-    for t in range(2):
-        shared_part(t).wait_send()
+    for t in range(SHARED // 2 - 2, SHARED // 2):
+        shared_part(jnp.int32(t)).wait_send()
     stage[...] = jnp.zeros((4, 4, ROW, CHUNK), jnp.float32)
 
     def second_step(i, carry):
@@ -376,7 +382,7 @@
             a_outer(u).wait_send()
         return carry
 
-    lax.fori_loop(0, 4, drain_solo, 0)
+    lax.fori_loop(0, SOLO // 2, drain_solo, 0)
 
     @pl.when(has_near)
     def _():
@@ -386,7 +392,7 @@
     for i, exists in enumerate((has_top, has_bot)):
         @pl.when(exists)
         def _():
-            for t in range(2):
+            for t in range(SHARED // 2):
                 a_halo(i, t).wait_send()
 
 
@@ -409,7 +415,7 @@
             scratch_shapes=[
                 pltpu.VMEM((6, ROW, half_o), bf16),
                 pltpu.VMEM((4, 6, ROW, CHUNK), bf16),
-                pltpu.VMEM((4, 2, ROW, CHUNK), bf16),
+                pltpu.VMEM((SOLO // 2, 2, ROW, CHUNK), bf16),
                 pltpu.VMEM((SLOTS, 3, 3, KBLOCK, CHUNK), bf16),
                 pltpu.VMEM((4, 4, ROW, CHUNK), f32),
                 pltpu.VMEM((8, 2, ROW, CHUNK), f32),
@@ -417,8 +423,8 @@
                 pltpu.VMEM((2, 2, ROW, CHUNK), f32),
                 pltpu.VMEM((2, 2, ROW, CHUNK), f32),
                 pltpu.VMEM((2 * half_h // 128, 128), f32),
-                dma((SLOTS, 3)), dma((2,)), dma, dma((4,)), dma((4,)), dma((2,)), dma((6,)), dma((2, 2)), dma((2, 2)),
-                dma((4,)), dma((2,)), dma((4,)), dma((2, 2)), dma((2, 4)), dma((2,)), dma((2,)),
+                dma((SLOTS, 3)), dma((2,)), dma, dma((4,)), dma((4,)), dma((2,)), dma(((SOLO + SHARED) // 2,)), dma((2, 2)), dma((2, 2)),
+                dma((SOLO // 2,)), dma((SOLO // 4,)), dma((SOLO // 2,)), dma((2, SHARED // 2)), dma((2, 4)), dma((2,)), dma((2,)),
             ],
             compiler_params=pltpu.CompilerParams(
                 collective_id=0, has_side_effects=True, vmem_limit_bytes=53 * 1024 * 1024),

time: 87.9 us -> 88.6 us (level)
  no operation moved by 1% of the time
where the time goes in v4:
time: 88.6 us; the launch traced here: 88.4 us
  Pallas kernels  85.3 us (96%)
  local copies, waits for them, and re-layouts  3.1 us (3%)
    pallas_call x1, Pallas kernels, local_block(): pl.pallas_call(functools.partial(resblock_kernel, sp_size, half_o, half_h...  85.3 us

profile of v4, /device:TPU:96, one launch (start us, length us, event | category | flops | bytes accessed | tf_op | source)
XLA Modules:
  0.0 88.4 jit_solution(9205259483960420476)
XLA Ops:
  0.0 1.1 %copy.5 = bf16[2,7,16,1024]{3,2,1,0:T(8,128)(2,1)S(1)} copy(bf16[2,7,16,1024]{3,0,1,2:T(2,128)(2,1)} %bitcast.10) | data formatting | bytes 917504 | tf_op jit(solution)/shard_map/transpose | solution.py:406
  1.1 0.0 copy-start
  1.1 0.7 copy-done
  1.9 85.3 %shard_map.46 = bf16[224,1024]{1,0:T(8,128)(2,1)S(1)} custom-call(bf16[224,1024]{1,0:T(8,128)(2,1)S(1)} %bitcast.8, bf16[3,3,1024,8192]{3,2,1,0:T(8,128)(2,1)} %w1_ref.1, bf16[3,3,4096,2048]{3,2,1,0:T(8,128)(2,1)} %w2_ref.1, f32[64,128]{1,0:T(8,128)S(1)} %bitcast.9), custom_call_target="tpu_custom_call" | custom-call | tf_op jit(solution)/shard_map/pallas_call | solution.py:410
  87.2 1.2 %copy.8 = bf16[2,7,16,1024]{3,0,1,2:T(2,128)(2,1)} copy(bf16[2,7,16,1024]{3,2,1,0:T(8,128)(2,1)S(1)} %bitcast.7) | data formatting | bytes 917504 | tf_op jit(solution)/shard_map/reshape | solution.py:432
Async XLA Ops:
  1.1 0.8 copy-start

commit v5 on v4

--- a/solution.py
+++ b/solution.py
@@ -38,6 +38,7 @@
     has_bot = q < sp_size // 2 - 1
     has_near = (s > 0) & (s < sp_size - 1)
     near_q = q + 2 * p - 1
+    share = lax.rem(p + q, 2)
 
     def w_copy(ref, kx, rows, cols, slot):
         return pltpu.make_async_copy(
@@ -51,7 +52,7 @@
             side = lax.rem(g, 2)
             u = g // 2
             shared = (g + SECOND - SOLO) // SECOND
-            unit = (1 - shared) * (UNITS * lax.rem(u, 2) + u // 2) + shared * (UNITS * p + u - SOLO // 4)
+            unit = (1 - shared) * (UNITS * lax.rem(u, 2) + u // 2) + shared * (UNITS * share + u - SOLO // 4)
             cols = (side * c + (1 - side) * other) * half_h + unit * CHUNK
             for kx, _, _, _ in TAPS:
                 w_copy(w1_ref, kx, 0, pl.multiple_of(cols, CHUNK), slot).start()
@@ -63,7 +64,7 @@
             m = lax.rem(t, 4) // 2
             side = lax.rem(t, 2)
             cols = (side * c + (1 - side) * other) * half_o + m * CHUNK
-            rows = p * 2 * KBLOCK + kb * KBLOCK
+            rows = share * 2 * KBLOCK + kb * KBLOCK
             for kx, _, _, _ in TAPS:
                 w_copy(w2_ref, kx, pl.multiple_of(rows, KBLOCK), pl.multiple_of(cols, CHUNK), slot).start()
 
@@ -74,9 +75,12 @@
         row = 1 - p if i == 0 else p
         return remote(x_ref.at[pl.ds(row * ROW, ROW)], xbuf.at[1 + 2 * p + row], xs_sem.at[i], xr_sem.at[i], {"sp": mate})
 
-    def x_outer(k):
-        return remote(x_ref.at[pl.ds(p * ROW, ROW)], xbuf.at[5 * (1 - p)], xs_sem.at[2 + k], xr_sem.at[3 - p],
-                      {"sp": 2 * near_q + k})
+    def x_outer():
+        return remote(x_ref.at[pl.ds(p * ROW, ROW)], xbuf.at[5 * (1 - p)], xs_sem.at[2], xr_sem.at[3 - p],
+                      {"sp": 2 * near_q + 1 - p})
+
+    def x_forward():
+        return remote(xbuf.at[5 * p], xbuf.at[5 * p], xs_sem.at[3], xr_sem.at[2 + p], {"sp": mate})
 
     def x_arrived(i):
         return remote(x_ref.at[pl.ds(0, ROW)], xbuf.at[0], xs_sem.at[0], xr_sem.at[i], {"sp": mate})
@@ -104,12 +108,13 @@
 
     def a_outer(u):
         k, j = unit_home(u)
-        return remote(asend.at[u, p], abuf.at[j, 5 * (1 - p)], os_sem.at[u], hr_sem.at[1 - p, j], {"sp": 2 * near_q + k})
+        return remote(asend.at[u, p], abuf.at[j, 5 * (1 - p)], os_sem.at[u], hr_sem.at[1 - p, j],
+                      {"sp": 2 * near_q + lax.rem(k + near_q, 2)})
 
     def a_halo(i, t):
         j = SOLO // 4 + t
         return remote(abuf.at[j, 1 + 3 * i], abuf.at[j, 5 * (1 - i)], hs_sem.at[i, t], hr_sem.at[1 - i, j],
-                      {"sp": lax.rem(s + sp_size + 4 * i - 2, sp_size)})
+                      {"sp": s - 2 * p - 1 + 4 * i})
 
     def halo_arrived(i, j):
         return remote(abuf.at[0, 0], abuf.at[j, 5 * i], hs_sem.at[0, 0], hr_sem.at[i, j], {"sp": mate})
@@ -141,21 +146,18 @@
 
     @pl.when(has_far)
     def _():
-        greet({"sp": s + 2 - 4 * p})
-
-    pl.semaphore_wait(barrier, 2 + 2 * has_near.astype(jnp.int32) + has_far.astype(jnp.int32))
+        for k in range(2):
+            greet({"sp": s + (2 + k) * (1 - 2 * p)})
+
+    pl.semaphore_wait(barrier, 2 + 2 * has_near.astype(jnp.int32) + 2 * has_far.astype(jnp.int32))
 
     x_mate(0).start()
 
     @pl.when(has_near)
     def _():
-        x_outer(1 - p).start()
+        x_outer().start()
 
     x_mate(1).start()
-
-    @pl.when(has_near)
-    def _():
-        x_outer(p).start()
 
     zero = jnp.zeros((ROW, CHUNK), jnp.bfloat16)
 
@@ -216,6 +218,7 @@
             @pl.when(has_near)
             def _():
                 x_arrived(2 + p).wait_recv()
+                x_forward().start()
 
         group(lax.rem(g, SLOTS), x_lhs, 2 * p, 2, stage.at[dst], 0, False)
         fetch(g + SLOTS)
@@ -234,11 +237,11 @@
                     val = stage[2, h, :, cols] + recv1[u, h, :, cols] + bias_row(UNITS * k + j, n)
                     asend[u, h, :, cols] = jnp.maximum(val, 0.0).astype(jnp.bfloat16)
 
-            @pl.when(k == p)
+            @pl.when(k == share)
             def _():
                 abuf[j, pl.ds(1 + 2 * p, 2)] = asend[u]
 
-            @pl.when(k != p)
+            @pl.when(k != share)
             def _():
                 a_mate(u).start()
 
@@ -281,7 +284,7 @@
             for r in range(4):
                 for n in range(CHUNK // 128):
                     cols = pl.ds(n * 128, 128)
-                    val = stage[2, r, :, cols] + recv1[SOLO // 2 + 2 * t + r // 2, r % 2, :, cols] + bias_row(UNITS * p + SOLO // 4 + t, n)
+                    val = stage[2, r, :, cols] + recv1[SOLO // 2 + 2 * t + r // 2, r % 2, :, cols] + bias_row(UNITS * share + SOLO // 4 + t, n)
                     abuf[SOLO // 4 + t, 1 + r, :, cols] = jnp.maximum(val, 0.0).astype(jnp.bfloat16)
 
             @pl.when(has_top)
@@ -373,7 +376,7 @@
     def drain_solo(u, carry):
         k, _ = unit_home(u)
 
-        @pl.when(k != p)
+        @pl.when(k != share)
         def _():
             a_mate(u).wait_send()
 
@@ -386,8 +389,8 @@
 
     @pl.when(has_near)
     def _():
-        for k in range(2):
-            x_outer(k).wait_send()
+        x_outer().wait_send()
+        x_forward().wait_send()
 
     for i, exists in enumerate((has_top, has_bot)):
         @pl.when(exists)

time: 88.6 us -> 88.2 us (level)
  no operation moved by 1% of the time
where the time goes in v5:
time: 88.2 us; the launch traced here: 88 us
  Pallas kernels  84.9 us (96%)
  local copies, waits for them, and re-layouts  3.1 us (4%)
    pallas_call x1, Pallas kernels, local_block(): pl.pallas_call(functools.partial(resblock_kernel, sp_size, half_o, half_h...  84.9 us

profile of v5, /device:TPU:96, one launch (start us, length us, event | category | flops | bytes accessed | tf_op | source)
XLA Modules:
  0.0 88.0 jit_solution(14348457990360033348)
XLA Ops:
  0.0 1.1 %copy.5 = bf16[2,7,16,1024]{3,2,1,0:T(8,128)(2,1)S(1)} copy(bf16[2,7,16,1024]{3,0,1,2:T(2,128)(2,1)} %bitcast.10) | data formatting | bytes 917504 | tf_op jit(solution)/shard_map/transpose | solution.py:409
  1.1 0.0 copy-start
  1.1 0.7 copy-done
  1.9 84.9 %shard_map.46 = bf16[224,1024]{1,0:T(8,128)(2,1)S(1)} custom-call(bf16[224,1024]{1,0:T(8,128)(2,1)S(1)} %bitcast.8, bf16[3,3,1024,8192]{3,2,1,0:T(8,128)(2,1)} %w1_ref.1, bf16[3,3,4096,2048]{3,2,1,0:T(8,128)(2,1)} %w2_ref.1, f32[64,128]{1,0:T(8,128)S(1)} %bitcast.9), custom_call_target="tpu_custom_call" | custom-call | tf_op jit(solution)/shard_map/pallas_call | solution.py:413
  86.8 1.2 %copy.8 = bf16[2,7,16,1024]{3,0,1,2:T(2,128)(2,1)} copy(bf16[2,7,16,1024]{3,2,1,0:T(8,128)(2,1)S(1)} %bitcast.7) | data formatting | bytes 917504 | tf_op jit(solution)/shard_map/reshape | solution.py:435
Async XLA Ops:
  1.1 0.8 copy-start

commit v6 on v5

--- a/solution.py
+++ b/solution.py
@@ -55,7 +55,7 @@
             unit = (1 - shared) * (UNITS * lax.rem(u, 2) + u // 2) + shared * (UNITS * share + u - SOLO // 4)
             cols = (side * c + (1 - side) * other) * half_h + unit * CHUNK
             for kx, _, _, _ in TAPS:
-                w_copy(w1_ref, kx, 0, pl.multiple_of(cols, CHUNK), slot).start()
+                w_copy(w1_ref, kx, 0, pl.multiple_of(cols, CHUNK), slot).start(priority=1)
 
         @pl.when((g >= SECOND) & (g < GROUPS))
         def _():
@@ -66,7 +66,7 @@
             cols = (side * c + (1 - side) * other) * half_o + m * CHUNK
             rows = share * 2 * KBLOCK + kb * KBLOCK
             for kx, _, _, _ in TAPS:
-                w_copy(w2_ref, kx, pl.multiple_of(rows, KBLOCK), pl.multiple_of(cols, CHUNK), slot).start()
+                w_copy(w2_ref, kx, pl.multiple_of(rows, KBLOCK), pl.multiple_of(cols, CHUNK), slot).start(priority=1)
 
     def remote(src, dst, send_sem, recv_sem, device_id):
         return pltpu.make_async_remote_copy(src, dst, send_sem, recv_sem, device_id=device_id, device_id_type=MESH)
@@ -122,13 +122,13 @@
     def mate_sum(m):
         return remote(msend.at[m], mrecv.at[m], ms_sem.at[m], mr_sem.at[m], {"sp": mate})
 
-    for g in range(SLOTS):
-        fetch(jnp.int32(g))
     x_copies = [pltpu.make_async_copy(x_ref.at[pl.ds(h * ROW, ROW)], xbuf.at[1 + 2 * p + h], xsem.at[h]) for h in range(2)]
     for x_copy in x_copies:
         x_copy.start()
     b_copy = pltpu.make_async_copy(bias_ref, bias_v, bsem)
     b_copy.start()
+    for g in range(SLOTS):
+        fetch(jnp.int32(g))
 
     has_far = ((p == 0) & has_bot) | ((p == 1) & has_top)
     barrier = pltpu.get_barrier_semaphore()

time: 88.2 us -> 88.2 us (level)
  no operation moved by 1% of the time
where the time goes in v6:
time: 88.2 us; the launch traced here: 88 us
  Pallas kernels  84.9 us (96%)
  local copies, waits for them, and re-layouts  3.1 us (4%)
    pallas_call x1, Pallas kernels, local_block(): pl.pallas_call(functools.partial(resblock_kernel, sp_size, half_o, half_h...  84.9 us

profile of v6, /device:TPU:96, one launch (start us, length us, event | category | flops | bytes accessed | tf_op | source)
XLA Modules:
  0.0 88.0 jit_solution(15650825204573553118)
XLA Ops:
  0.0 1.1 %copy.5 = bf16[2,7,16,1024]{3,2,1,0:T(8,128)(2,1)S(1)} copy(bf16[2,7,16,1024]{3,0,1,2:T(2,128)(2,1)} %bitcast.10) | data formatting | bytes 917504 | tf_op jit(solution)/shard_map/transpose | solution.py:409
  1.1 0.0 copy-start
  1.1 0.7 copy-done
  1.9 84.9 %shard_map.46 = bf16[224,1024]{1,0:T(8,128)(2,1)S(1)} custom-call(bf16[224,1024]{1,0:T(8,128)(2,1)S(1)} %bitcast.8, bf16[3,3,1024,8192]{3,2,1,0:T(8,128)(2,1)} %w1_ref.1, bf16[3,3,4096,2048]{3,2,1,0:T(8,128)(2,1)} %w2_ref.1, f32[64,128]{1,0:T(8,128)S(1)} %bitcast.9), custom_call_target="tpu_custom_call" | custom-call | tf_op jit(solution)/shard_map/pallas_call | solution.py:413
  86.8 1.2 %copy.8 = bf16[2,7,16,1024]{3,0,1,2:T(2,128)(2,1)} copy(bf16[2,7,16,1024]{3,2,1,0:T(8,128)(2,1)S(1)} %bitcast.7) | data formatting | bytes 917504 | tf_op jit(solution)/shard_map/reshape | solution.py:435
Async XLA Ops:
  1.1 0.8 copy-start
